TPU v7x, 32 devices: a whole 2x2x4 slice. The times are simulated.
32 devices in a mesh: dom: 16 (over z, y, x), mp: 2 (over core).
Axes of the slice: x: 2, y: 2, z: 4, core: 2. Of those that a mesh axis runs over, the one named last changes fastest.
Arguments:
- table: bfloat16 [65536, 768], P('dom', 'mp'), may hold values from -6 to 6
- weight_a: bfloat16 [1536, 512], P(None, 'mp'), may hold values from -0.15625 to 0.15625
- bias_a: float32 [512], replicated, may hold values from -3 to 3
- weight_b: bfloat16 [1024, 512], P(None, 'mp'), may hold values from -0.25 to 0.25
- bias_b: float32 [512], replicated, may hold values from -3 to 3
- requests: int32 [16, 16, 128], P('dom'), may hold values from 0 to 4095
- near_a: int32 [16384, 10], P('dom'), may hold values from 0 to 2047
- self_a: int32 [16384], P('dom'), may hold values from 0 to 2047
- count_a: int32 [16384], P('dom'), may hold values from 1 to 10
- near_b: int32 [4096, 5], P('dom'), may hold values from 0 to 1023
- self_b: int32 [4096], P('dom'), may hold values from 0 to 1023
- count_b: int32 [4096], P('dom'), may hold values from 1 to 5
Outputs:
- embedding: bfloat16 [4096, 512], P('dom', 'mp')
Inputs may be any that keep to these rules, and one draw needn't show every extreme that they name: `requests`: local row indices at the owner. `near_a`: slots of the same minibatch; entries at j >= count_a are padding. `near_b`: positions within the same minibatch; entries at j >= count_b are padding.
All inputs are finite; a program needn't handle non-finite values.
Results may differ from a plain program's by a relative error of at most 0.0074.
Values may be sent and summed in bfloat16 or wider, within the bound.
A program may use at most 64 MiB of HBM per device.

v0:
```python
import functools

import jax
import jax.numpy as jnp
from jax import lax
from jax.experimental import pallas as pl
from jax.experimental.pallas import tpu as pltpu
from jax.sharding import PartitionSpec as P

MESH = pl.DeviceIdType.MESH
VMEM = pl.BlockSpec(memory_space=pltpu.VMEM)
TILE = 256


def peer(me, step, n):
    if n & (n - 1):
        return lax.rem(me + 1 + lax.rem(n // 2 - 1 + step, n - 1), n)
    return exchanged(me, n - 1 - step, n)


def exchanged(me, mask, n):
    other, bit = 0, 1
    while bit < n:
        other = other + lax.rem(me // bit + mask // bit, 2) * bit
        bit *= 2
    return other


def greet(me, n, partner):
    barrier = pltpu.get_barrier_semaphore()

    def one(step, carry):
        pl.semaphore_signal(
            barrier, inc=1, device_id={"dom": peer(me, step, n)}, device_id_type=MESH
        )
        return carry

    lax.fori_loop(0, n - 1, one, 0)
    if partner is not None:
        pl.semaphore_signal(barrier, inc=1, device_id={"mp": partner}, device_id_type=MESH)
    pl.semaphore_wait(barrier, n - 1 + (partner is not None))


def block_copy(source, landed, me, other, send_sem, recv_sem):
    return pltpu.make_async_remote_copy(
        src_ref=source.at[other],
        dst_ref=landed.at[me],
        send_sem=send_sem.at[other],
        recv_sem=recv_sem.at[me],
        device_id={"dom": other},
        device_id_type=MESH,
    )


def send_blocks(source, landed, me, n, send_sem, recv_sem):
    def one(step, carry):
        block_copy(source, landed, me, peer(me, step, n), send_sem, recv_sem).start()
        return carry

    lax.fori_loop(0, n - 1, one, 0)


def finish_sends(source, landed, me, n, send_sem, recv_sem):
    def one(step, carry):
        block_copy(source, landed, me, peer(me, step, n), send_sem, recv_sem).wait_send()
        return carry

    lax.fori_loop(0, n - 1, one, 0)


def wait_block(source, landed, other, recv_sem):
    pltpu.make_async_copy(source.at[other], landed.at[other], recv_sem.at[other]).wait()


def build_picks(index_ref, fan, mean_pick, own_pick):
    rows, columns = mean_pick.shape
    high = 16
    short = jnp.int16 if columns < 2**15 else jnp.int32

    def one(at, carry):
        r0 = pl.multiple_of(at * high, high)
        index = index_ref[pl.ds(r0, high), :]
        lanes = [
            jnp.broadcast_to(index[:, j : j + 1], (high, 128)).astype(short)
            for j in range(fan + 1)
        ]
        lane = lax.broadcasted_iota(jnp.int32, (high, 128), 1)
        one_value, no_value = jnp.bfloat16(1.0), jnp.bfloat16(0.0)
        for c in range(0, columns, 128):
            column = (lane + c).astype(short)
            total = jnp.where(lanes[0] == column, one_value, no_value)
            for j in range(1, fan):
                total = total + jnp.where(lanes[j] == column, one_value, no_value)
            mean_pick[pl.ds(r0, high), c : c + 128] = total
            own_pick[pl.ds(r0, high), c : c + 128] = jnp.where(
                lanes[fan] == column, one_value, no_value
            )
        return carry

    lax.fori_loop(0, rows // high, one, 0)


def dot(a, b):
    return jnp.dot(a, b, preferred_element_type=jnp.float32)


def index_rows(index, near_ref, own_ref, count_ref):
    fan, rows = near_ref.shape
    count = count_ref[...]
    pieces = [jnp.where(count > j, near_ref[j : j + 1, :], -1) for j in range(fan)]
    pieces += [own_ref[...], count, jnp.zeros((index.shape[1] - fan - 2, rows), jnp.int32)]
    index[...] = jnp.concatenate(pieces, axis=0).T


def main_kernel(
    n,
    asked_ref, table_ref, near_a_ref, self_a_ref, count_a_ref, near_b_ref, self_b_ref, count_b_ref,
    weight_a_any, bias_a_ref, weight_b_any, bias_b_ref,
    out_ref,
    table, table_wide, wanted, wanted_scalar, stage, found_ref,
    weight_a_ref, weight_b_ref, index_a_ref, index_b_ref,
    fetched, pick_a, self_pick_a, pick_b, self_pick_b, sum_mean, sum_own,
    mine_a, theirs_a, hidden, mine_b, theirs_b, mine_sq, theirs_sq,
    ask_send, ask_recv, send_sem, recv_sem, mp_send, mp_recv, load_sem, scalar_sem,
):
    me = lax.axis_index("dom")
    core = lax.axis_index("mp")
    partner = 1 - core
    each, half = found_ref.shape[1], found_ref.shape[2]
    rows = sum_mean.shape[0]
    half_hidden = hidden.shape[1]
    feature, hidden_width = weight_a_ref.shape[0] // 2, weight_b_ref.shape[0] // 2
    fan_a, fan_b = near_a_ref.shape[0], near_b_ref.shape[0]

    load_table = pltpu.make_async_copy(table_ref, table, load_sem.at[0])
    load_table.start()
    greet(me, n, partner)
    send_blocks(asked_ref, wanted, me, n, ask_send, ask_recv)
    pltpu.make_async_copy(asked_ref.at[me], wanted.at[me], ask_recv.at[me]).start()
    load_table.wait()
    load_a = pltpu.make_async_copy(weight_a_any, weight_a_ref, load_sem.at[1])
    load_a.start()
    load_b = pltpu.make_async_copy(weight_b_any, weight_b_ref, load_sem.at[2])
    load_b.start()

    def widen(tile, carry):
        at = pl.ds(pl.multiple_of(tile * 128, 128), 128)
        table_wide[at, :] = table[at, :].astype(jnp.float32)
        return carry

    lax.fori_loop(0, table.shape[0] // 128, widen, 0)
    index_rows(index_a_ref, near_a_ref, self_a_ref, count_a_ref)
    index_rows(index_b_ref, near_b_ref, self_b_ref, count_b_ref)

    def to_scalar(other):
        return pltpu.make_async_copy(wanted.at[other], wanted_scalar.at[other], scalar_sem.at[other])

    def find(other):
        to_scalar(other).wait()

        def some(at, carry):
            r0 = at * 16
            for k in range(16):
                row = wanted_scalar[other, 0, r0 + k]
                stage[pl.ds(r0 + k, 1), :] = table_wide[pl.ds(row, 1), :]
            return carry

        lax.fori_loop(0, each // 16, some, 0)
        found_ref[other] = stage[...].astype(jnp.bfloat16)

    behind = min(2, n - 1)

    def asked_of(step):
        other = peer(me, step, n)
        wait_block(asked_ref, wanted, other, ask_recv)
        to_scalar(other).start()

    def find_and_send(step, carry):
        @pl.when(step < n - 1)
        def _():
            asked_of(step)

        @pl.when(step >= behind)
        def _():
            other = peer(me, step - behind, n)
            find(other)
            block_copy(found_ref, fetched, me, other, send_sem, recv_sem).start()

        return carry

    lax.fori_loop(0, n - 1 + behind, find_and_send, 0)
    wait_block(asked_ref, wanted, me, ask_recv)
    to_scalar(me).start()
    find(me)
    pltpu.make_async_copy(found_ref.at[me], fetched.at[me], recv_sem.at[me]).start()
    build_picks(index_a_ref, fan_a, pick_a, self_pick_a)
    build_picks(index_b_ref, fan_b, pick_b, self_pick_b)
    sum_mean[...] = jnp.zeros_like(sum_mean)
    sum_own[...] = jnp.zeros_like(sum_own)
    mine_cols = pl.ds(pl.multiple_of(core * half_hidden, 128), half_hidden)
    load_a.wait()
    load_b.wait()

    per = min(n, max(1, 256 // each))
    groups = n // per
    depth = per * each

    def one_group(step, carry):
        group = exchanged(me // per, lax.rem(groups - step, groups), groups)

        def arrive(i, inner):
            wait_block(found_ref, fetched, group * per + i, recv_sem)
            return inner

        lax.fori_loop(0, per, arrive, 0)
        columns = pl.ds(pl.multiple_of(group * depth, depth), depth)

        def one_tile(tile, inner):
            at = pl.ds(pl.multiple_of(tile * TILE, TILE), TILE)
            block = fetched[pl.ds(group * per, per)].reshape(depth, half)
            sum_mean[at, :] += dot(pick_a[at, columns], block)
            sum_own[at, :] += dot(self_pick_a[at, columns], block)
            return inner

        lax.fori_loop(0, rows // TILE, one_tile, 0)
        return carry

    lax.fori_loop(0, groups, one_group, 0)

    def swap(source, landed, at):
        return pltpu.make_async_remote_copy(
            src_ref=source,
            dst_ref=landed,
            send_sem=mp_send.at[at],
            recv_sem=mp_recv.at[at],
            device_id={"mp": partner},
            device_id_type=MESH,
        )

    def rows_of(weight_ref, start, width, which):
        return weight_ref[pl.ds(pl.multiple_of(start + which * width, 128), width), :]

    def swap_a(tile):
        return swap(mine_a.at[tile], theirs_a.at[tile], 2 + tile)

    def layer_a(tile, carry):
        at = pl.ds(pl.multiple_of(tile * TILE, TILE), TILE)
        count = index_a_ref[at, fan_a + 1 : fan_a + 2].astype(jnp.float32)
        mine_a[tile, 0] = sum_own[at, :].astype(jnp.bfloat16)
        mine_a[tile, 1] = (sum_mean[at, :] / count).astype(jnp.bfloat16)
        swap_a(tile).start()
        value = dot(mine_a[tile, 0], rows_of(weight_a_ref, 0, half, core))
        value = value + dot(mine_a[tile, 1], rows_of(weight_a_ref, feature, half, core))
        sum_own[at, pl.ds(0, half_hidden)] = value
        return carry

    def layer_a_rest(tile, carry):
        at = pl.ds(pl.multiple_of(tile * TILE, TILE), TILE)
        swap_a(tile).wait()
        value = sum_own[at, pl.ds(0, half_hidden)]
        value = value + dot(theirs_a[tile, 0], rows_of(weight_a_ref, 0, half, partner))
        value = value + dot(theirs_a[tile, 1], rows_of(weight_a_ref, feature, half, partner))
        hidden[at, :] = jnp.maximum(value + bias_a_ref[:, mine_cols], 0.0).astype(jnp.bfloat16)
        return carry

    lax.fori_loop(0, rows // TILE, layer_a, 0)
    lax.fori_loop(0, rows // TILE, layer_a_rest, 0)

    mine_b[0] = dot(self_pick_b[...], hidden[...]).astype(jnp.bfloat16)
    count_b = index_b_ref[:, fan_b + 1 : fan_b + 2].astype(jnp.float32)
    mine_b[1] = (dot(pick_b[...], hidden[...]) / count_b).astype(jnp.bfloat16)
    swap_b = swap(mine_b, theirs_b, 0)
    swap_b.start()
    state = dot(mine_b[0], rows_of(weight_b_ref, 0, half_hidden, core))
    state = state + dot(mine_b[1], rows_of(weight_b_ref, hidden_width, half_hidden, core))
    swap_b.wait()
    state = state + dot(theirs_b[0], rows_of(weight_b_ref, 0, half_hidden, partner))
    state = state + dot(theirs_b[1], rows_of(weight_b_ref, hidden_width, half_hidden, partner))
    state = jnp.maximum(state + bias_b_ref[:, mine_cols], 0.0)
    mine_sq[...] = jnp.broadcast_to(jnp.sum(state * state, axis=1, keepdims=True), mine_sq.shape)
    swap_sq = swap(mine_sq, theirs_sq, 1)
    swap_sq.start()
    swap_sq.wait()
    squares = mine_sq[:, 0:1] + theirs_sq[:, 0:1]
    scale = jnp.sqrt(jnp.float32(hidden_width)) / jnp.sqrt(squares + hidden_width)
    out_ref[...] = (state * scale).astype(out_ref.dtype)
    finish_sends(asked_ref, wanted, me, n, ask_send, ask_recv)
    finish_sends(found_ref, fetched, me, n, send_sem, recv_sem)


def shards(
    n,
    table,
    weight_a,
    bias_a,
    weight_b,
    bias_b,
    requests,
    near_a,
    self_a,
    count_a,
    near_b,
    self_b,
    count_b,
):
    each = requests.shape[2]
    half, half_hidden = table.shape[1], weight_a.shape[1]
    rows, seeds, slots = near_a.shape[0], near_b.shape[0], n * each
    wide = -(-(near_a.shape[1] + 2) // 8) * 8
    bf16, f32 = jnp.bfloat16, jnp.float32
    anywhere = pl.BlockSpec(memory_space=pl.ANY)
    return pl.pallas_call(
        functools.partial(main_kernel, n),
        out_shape=jax.ShapeDtypeStruct((seeds, half_hidden), bf16),
        in_specs=[VMEM, anywhere] + [VMEM] * 6 + [anywhere, VMEM, anywhere, VMEM],
        out_specs=VMEM,
        scratch_shapes=[
            pltpu.VMEM(table.shape, bf16),
            pltpu.VMEM(table.shape, f32),
            pltpu.VMEM((n, 1, each), jnp.int32),
            pltpu.SMEM((n, 1, each), jnp.int32),
            pltpu.VMEM((each, half), f32),
            pltpu.VMEM((n, each, half), bf16),
            pltpu.VMEM(weight_a.shape, bf16),
            pltpu.VMEM(weight_b.shape, bf16),
            pltpu.VMEM((rows, wide), jnp.int32),
            pltpu.VMEM((seeds, wide), jnp.int32),
            pltpu.VMEM((n, each, half), bf16),
            pltpu.VMEM((rows, slots), bf16),
            pltpu.VMEM((rows, slots), bf16),
            pltpu.VMEM((seeds, rows), bf16),
            pltpu.VMEM((seeds, rows), bf16),
            pltpu.VMEM((rows, half), f32),
            pltpu.VMEM((rows, half), f32),
            pltpu.VMEM((rows // TILE, 2, TILE, half), bf16),
            pltpu.VMEM((rows // TILE, 2, TILE, half), bf16),
            pltpu.VMEM((rows, half_hidden), bf16),
            pltpu.VMEM((2, seeds, half_hidden), bf16),
            pltpu.VMEM((2, seeds, half_hidden), bf16),
            pltpu.VMEM((seeds, 128), f32),
            pltpu.VMEM((seeds, 128), f32),
            pltpu.SemaphoreType.DMA((n,)),
            pltpu.SemaphoreType.DMA((n,)),
            pltpu.SemaphoreType.DMA((n,)),
            pltpu.SemaphoreType.DMA((n,)),
            pltpu.SemaphoreType.DMA((2 + rows // TILE,)),
            pltpu.SemaphoreType.DMA((2 + rows // TILE,)),
            pltpu.SemaphoreType.DMA((3,)),
            pltpu.SemaphoreType.DMA((n,)),
        ],
        compiler_params=pltpu.CompilerParams(
            collective_id=0, has_side_effects=True, vmem_limit_bytes=60 * 1024 * 1024
        ),
        name="sage",
    )(
        requests[0][:, None, :], table,
        near_a.T, self_a[None, :], count_a[None, :], near_b.T, self_b[None, :], count_b[None, :],
        weight_a, bias_a[None, :], weight_b, bias_b[None, :],
    )


def solution(mesh):
    placed = (
        P("dom", "mp"),
        P(None, "mp"),
        P(),
        P(None, "mp"),
        P(),
        P("dom", None, None),
        P("dom", None),
        P("dom"),
        P("dom"),
        P("dom", None),
        P("dom"),
        P("dom"),
    )
    return jax.shard_map(
        functools.partial(shards, mesh.shape["dom"]),
        mesh=mesh, in_specs=placed, out_specs=P("dom", "mp"), check_vma=False,
    )
```

profile of v0, /device:TPU:0, one launch (start us, length us, event | category | flops | bytes accessed | tf_op | source)
XLA Modules:
  0.0 61.5 jit_solution(17760465620839810160)
XLA Ops:
  0.0 59.9 %sage.1 = bf16[256,256]{1,0:T(8,128)(2,1)} custom-call(s32[16,1,128]{2,1,0:T(1,128)} %bitcast.10, bf16[4096,384]{1,0:T(8,128)(2,1)} %table_ref.1, s32[10,1024]{1,0:T(8,128)} %bitcast.9, s32[1,1024]{1,0:T(1,128)} %bitcast.12, s32[1,1024]{1,0:T(1,128)} %bitcast.13, s32[5,256]{1,0:T(8,128)} %bitcast.11, s32[1,256]{1,0:T(1,128)} %bitcast.16, s32[1,256]{1,0:T(1,128)} %bitcast.17, ...), custom_call_target="tpu_custom_call" | custom-call | tf_op jit(solution)/shard_map/sage/pallas_call | solution.py:312
  59.9 1.6 %copy.14 = bf16[256,256]{1,0:T(8,128)(2,1)} copy(bf16[256,256]{1,0:T(8,128)(2,1)} %sage.1) | data formatting | bytes 262144
where the time goes:
time: 61.7 us; the launch traced here: 61.5 us
  Pallas kernels  59.9 us (97%)
  local copies, waits for them, and re-layouts  1.57 us (3%)
    pallas_call x1, Pallas kernels, shards(): pl.pallas_call(functools.partial(main_kernel, n), out_shape=jax.ShapeDtyp...  59.9 us
    unnamed x1, local copies, waits for them, and re-layouts  1.57 us

commit v1 on v0

v1 whole, which is shorter than its diff:
```python
import functools

import jax
import jax.numpy as jnp
from jax import lax
from jax.experimental import pallas as pl
from jax.experimental.pallas import tpu as pltpu
from jax.sharding import PartitionSpec as P

MESH = pl.DeviceIdType.MESH
VMEM = pl.BlockSpec(memory_space=pltpu.VMEM)
ANY = pl.BlockSpec(memory_space=pl.ANY)
LANE = 128
TILE = 256
DEPTH = 256


def bit(value, k):
    return lax.rem(lax.div(value, 2**k), 2)


def flips(me, n):
    return [2**k * (1 - 2 * bit(me, k)) for k in range((n - 1).bit_length())]


def exchanged(me, flip, mask):
    for k, delta in enumerate(flip):
        me = me + bit(mask, k) * delta
    return me


def mask_of(step, n):
    half = lax.div(step, 2)
    odd = lax.rem(step, 2)
    return (1 - odd) * (n // 2 + half) + odd * (half + 1)


def dot(a, b):
    return jnp.dot(a, b, preferred_element_type=jnp.float32)


def across(pieces):
    return jnp.concatenate(pieces, axis=1)


def index_rows(index, near_ref, own_ref, count_ref):
    fan, rows = near_ref.shape
    count = count_ref[...]
    pieces = [jnp.where(count > j, near_ref[j : j + 1, :], -1) for j in range(fan)]
    pieces += [own_ref[...], count, jnp.zeros((index.shape[1] - fan - 2, rows), jnp.int32)]
    index[...] = jnp.concatenate(pieces, axis=0).T


def build_picks(index_ref, fan, sum_pick, own_pick, inverse, scaled, first, last):
    chunks = sum_pick.shape[0]
    high = 16

    def one(at, carry):
        r0 = pl.multiple_of(at * high, high)
        index = index_ref[pl.ds(r0, high), :]
        lanes = [
            jnp.broadcast_to(index[:, j : j + 1], (high, LANE)).astype(jnp.int16)
            for j in range(fan + 1)
        ]
        count = jnp.broadcast_to(index[:, fan + 1 : fan + 2], (high, LANE)).astype(jnp.float32)
        inverse[pl.ds(r0, high), :] = 1.0 / count
        lane = lax.broadcasted_iota(jnp.int32, (high, LANE), 1)
        one_value, no_value = jnp.bfloat16(1.0), jnp.bfloat16(0.0)
        own_value = count.astype(jnp.bfloat16) if scaled else one_value
        for c in range(chunks):
            column = (lane + c * LANE).astype(jnp.int16)
            total = jnp.where(lanes[0] == column, one_value, no_value)
            for j in range(1, fan):
                total = total + jnp.where(lanes[j] == column, one_value, no_value)
            sum_pick[c, pl.ds(r0, high), :] = total
            own_pick[c, pl.ds(r0, high), :] = jnp.where(lanes[fan] == column, own_value, no_value)
        return carry

    lax.fori_loop(first, last, one, 0)


def main_kernel(
    n,
    asked_any, table_any, near_a_any, self_a_any, count_a_any, near_b_any, self_b_any, count_b_any,
    weight_a_any, bias_a_any, weight_b_any, bias_b_any,
    out_ref,
    asked, table, near_a, self_a, count_a, near_b, self_b, count_b, wa, bias_a, wb, bias_b,
    wide, wanted, wanted_scalar, stage, found, index_a, index_b,
    fetched, sum_a, own_a, sum_b, own_b, inv_a, inv_b, mixed, total, hidden,
    ask_send, ask_recv, send_sem, recv_sem, relay_send, relay_recv, mp_send, mp_recv, load_sem, scalar_sem,
):
    me = lax.axis_index("dom")
    core = lax.axis_index("mp")
    partner = 1 - core
    flip = flips(me, n)
    cols, each = found.shape[1], found.shape[2]
    rows, seeds, slots = inv_a.shape[0], inv_b.shape[0], n * each
    feature, hidden_width = wa.shape[1] // 2, wb.shape[1] // 2
    fan_a, fan_b = near_a.shape[0], near_b.shape[0]
    blocks = wa.shape[0] // 2
    per = max(1, DEPTH // each)
    groups = n // per
    depth = per * each
    deep = depth // LANE

    def peer(step):
        return exchanged(me, flip, mask_of(step, n))

    loads = [
        pltpu.make_async_copy(source, target, load_sem.at[i])
        for i, (source, target) in enumerate(
            [(asked_any, asked), (near_a_any, near_a), (self_a_any, self_a), (count_a_any, count_a),
             (near_b_any, near_b), (self_b_any, self_b), (count_b_any, count_b), (table_any, table),
             (bias_a_any, bias_a), (bias_b_any, bias_b)]
            + [(weight_a_any.at[:, pl.ds(i * LANE, LANE)], wa.at[core * blocks + i]) for i in range(blocks)]
            + [(weight_b_any.at[:, pl.ds(i * LANE, LANE)], wb.at[core * blocks + i]) for i in range(blocks)]
        )
    ]
    for load in loads:
        load.start()

    barrier = pltpu.get_barrier_semaphore()

    def greet(step, carry):
        pl.semaphore_signal(barrier, inc=1, device_id={"dom": peer(step)}, device_id_type=MESH)
        return carry

    lax.fori_loop(0, n - 1, greet, 0)
    pl.semaphore_signal(barrier, inc=1, device_id={"mp": partner}, device_id_type=MESH)

    for load in loads[1:7]:
        load.wait()
    index_rows(index_a, near_a, self_a, count_a)
    index_rows(index_b, near_b, self_b, count_b)
    steps = rows // 16
    build_picks(index_a, fan_a, sum_a, own_a, inv_a, True, 0, steps // 2)

    loads[0].wait()
    wanted[me] = asked[me]
    pl.semaphore_wait(barrier, n)

    def ask(other):
        return pltpu.make_async_remote_copy(
            src_ref=asked.at[other], dst_ref=wanted.at[me],
            send_sem=ask_send.at[other], recv_sem=ask_recv.at[me],
            device_id={"dom": other}, device_id_type=MESH,
        )

    def give(other):
        return pltpu.make_async_remote_copy(
            src_ref=found.at[other], dst_ref=fetched.at[core, me],
            send_sem=send_sem.at[other], recv_sem=recv_sem.at[me],
            device_id={"dom": other}, device_id_type=MESH,
        )

    def over(source, target, send, recv):
        return pltpu.make_async_remote_copy(
            src_ref=source, dst_ref=target, send_sem=send, recv_sem=recv,
            device_id={"mp": partner}, device_id_type=MESH,
        )

    def relay(other):
        return over(fetched.at[core, other], fetched.at[core, other], relay_send.at[other], relay_recv.at[other])

    def send_ask(step, carry):
        ask(peer(step)).start()
        return carry

    lax.fori_loop(0, n - 1, send_ask, 0)
    for load in loads[7:]:
        load.wait()
    shared = [
        over(w.at[core * blocks + i], w.at[core * blocks + i], mp_send.at[s * blocks + i], mp_recv.at[s * blocks + i])
        for s, w in enumerate((wa, wb)) for i in range(blocks)
    ]
    for copy in shared:
        copy.start()

    def widen(tile, carry):
        at = pl.ds(pl.multiple_of(tile * 128, 128), 128)
        for c in range(cols):
            wide[c, at, :] = table[at, c * LANE : (c + 1) * LANE].astype(jnp.float32)
        return carry

    lax.fori_loop(0, table.shape[0] // 128, widen, 0)
    build_picks(index_a, fan_a, sum_a, own_a, inv_a, True, steps // 2, steps)

    def to_scalar(other):
        return pltpu.make_async_copy(wanted.at[other], wanted_scalar.at[other], scalar_sem.at[other])

    def find(other):
        to_scalar(other).wait()
        for k in range(each):
            row = wanted_scalar[other, 0, k]
            for c in range(cols):
                stage[c, k : k + 1, :] = wide[c, pl.ds(row, 1), :]
        for c in range(cols):
            found[other, c] = stage[c].astype(jnp.bfloat16)

    behind = min(3, n)

    def step_peer(step):
        return exchanged(me, flip, jnp.where(step < n - 1, mask_of(step, n), 0))

    def find_and_send(step, carry):
        @pl.when(step < n)
        def _():
            other = step_peer(step)

            @pl.when(step < n - 1)
            def _():
                pltpu.make_async_copy(asked.at[other], wanted.at[other], ask_recv.at[other]).wait()

            to_scalar(other).start()

        @pl.when(step >= behind)
        def _():
            other = step_peer(step - behind)
            find(other)

            @pl.when(step - behind < n - 1)
            def _():
                give(other).start()

        return carry

    lax.fori_loop(0, n + behind, find_and_send, 0)
    fetched[core, me] = found[me]
    build_picks(index_b, fan_b, sum_b, own_b, inv_b, False, 0, seeds // 16)
    total[...] = jnp.zeros_like(total)
    relay(me).start()
    for copy in shared:
        copy.wait()

    group_flip = flips(lax.div(me, per), groups)
    half_groups = max(1, groups // 2)

    def group_of(k):
        j = lax.rem(k, 2) * half_groups + lax.div(k, 2)
        return exchanged(lax.div(me, per), group_flip, j)

    def take(group):
        def arrive(i, carry):
            other = group * per + i

            @pl.when(other != me)
            def _():
                pltpu.make_async_copy(found.at[other], fetched.at[core, other], recv_sem.at[other]).wait()
                relay(other).start()

            return carry

        lax.fori_loop(0, per, arrive, 0)

    def use(group):
        def arrive(i, carry):
            other = group * per + i
            pltpu.make_async_copy(found.at[other], fetched.at[partner, other], relay_recv.at[other]).wait()
            return carry

        lax.fori_loop(0, per, arrive, 0)
        lines = across([
            fetched[h, pl.ds(group * per, per), c].reshape(depth, LANE) for h in range(2) for c in range(cols)
        ])
        for which in range(2):
            at = pl.ds(which * feature, feature)
            for b in range(0, 2 * blocks, 2):
                value = dot(lines, across([wa[b, at, :], wa[b + 1, at, :]])).astype(jnp.bfloat16)
                for i in range(2):
                    mixed[b + i, which * depth : (which + 1) * depth, :] = value[:, i * LANE : (i + 1) * LANE]

        def one_tile(tile, carry):
            at = pl.ds(pl.multiple_of(tile * TILE, TILE), TILE)
            picks = across([p[group * deep + i, at, :] for p in (own_a, sum_a) for i in range(deep)])
            for b in range(blocks):
                total[b, at, :] += dot(picks, across([mixed[2 * b], mixed[2 * b + 1]]))
            return carry

        lax.fori_loop(0, rows // TILE, one_tile, 0)

    def one_group(k, carry):
        @pl.when(k < groups)
        def _():
            take(group_of(k))

        @pl.when(k > 0)
        def _():
            use(group_of(k - 1))

        return carry

    lax.fori_loop(0, groups + 1, one_group, 0)

    def hide(tile, carry):
        at = pl.ds(pl.multiple_of(tile * TILE, TILE), TILE)
        inverse = inv_a[at, :]
        for b in range(blocks):
            for i in range(2):
                cut = slice((2 * b + i) * LANE, (2 * b + i + 1) * LANE)
                value = total[b, at, i * LANE : (i + 1) * LANE] * inverse + bias_a[:, cut]
                hidden[2 * b + i, at, :] = jnp.maximum(value, 0.0).astype(jnp.bfloat16)
        return carry

    lax.fori_loop(0, rows // TILE, hide, 0)

    hidden_all = across([hidden[b] for b in range(2 * blocks)])
    chunks_b = own_b.shape[0]
    own = dot(across([own_b[c] for c in range(chunks_b)]), hidden_all).astype(jnp.bfloat16)
    mean = dot(across([sum_b[c] for c in range(chunks_b)]), hidden_all)
    mean = (mean * across([inv_b[...]] * (2 * blocks))).astype(jnp.bfloat16)
    state = dot(own, across([wb[b, :hidden_width] for b in range(2 * blocks)]))
    state = state + dot(mean, across([wb[b, hidden_width:] for b in range(2 * blocks)]))
    state = jnp.maximum(state + bias_b[...], 0.0)
    squares = jnp.sum(state * state, axis=1, keepdims=True)
    scale = jnp.sqrt(jnp.float32(hidden_width)) / jnp.sqrt(squares + hidden_width)
    state = (state * scale).astype(out_ref.dtype)
    half = out_ref.shape[1]
    for c in range(2):
        @pl.when(core == c)
        def _():
            out_ref[...] = state[:, c * half : (c + 1) * half]

    def finish(step, carry):
        other = peer(step)
        ask(other).wait_send()
        give(other).wait_send()
        relay(other).wait_send()
        return carry

    lax.fori_loop(0, n - 1, finish, 0)
    relay(me).wait_send()


def shards(
    n,
    table,
    weight_a,
    bias_a,
    weight_b,
    bias_b,
    requests,
    near_a,
    self_a,
    count_a,
    near_b,
    self_b,
    count_b,
):
    each = requests.shape[2]
    half, half_hidden = table.shape[1], weight_a.shape[1]
    rows, seeds, slots = near_a.shape[0], near_b.shape[0], n * each
    wide = -(-(near_a.shape[1] + 2) // 8) * 8
    bf16, f32 = jnp.bfloat16, jnp.float32
    cols, blocks = half // LANE, half_hidden // LANE
    depth = max(1, DEPTH // each) * each
    args = (
        requests[0][:, None, :], table,
        near_a.T, self_a[None, :], count_a[None, :], near_b.T, self_b[None, :], count_b[None, :],
        weight_a, bias_a[None, :], weight_b, bias_b[None, :],
    )
    return pl.pallas_call(
        functools.partial(main_kernel, n),
        out_shape=jax.ShapeDtypeStruct((seeds, half_hidden), bf16),
        in_specs=[ANY] * len(args),
        out_specs=VMEM,
        scratch_shapes=[pltpu.VMEM(a.shape, a.dtype) for a in args[:8]] + [
            pltpu.VMEM((2 * blocks, weight_a.shape[0], LANE), bf16),
            pltpu.VMEM(args[9].shape, f32),
            pltpu.VMEM((2 * blocks, weight_b.shape[0], LANE), bf16),
            pltpu.VMEM(args[11].shape, f32),
            pltpu.VMEM((cols, table.shape[0], LANE), f32),
            pltpu.VMEM((n, 1, each), jnp.int32),
            pltpu.SMEM((n, 1, each), jnp.int32),
            pltpu.VMEM((cols, each, LANE), f32),
            pltpu.VMEM((n, cols, each, LANE), bf16),
            pltpu.VMEM((rows, wide), jnp.int32),
            pltpu.VMEM((seeds, wide), jnp.int32),
            pltpu.VMEM((2, n, cols, each, LANE), bf16),
            pltpu.VMEM((slots // LANE, rows, LANE), bf16),
            pltpu.VMEM((slots // LANE, rows, LANE), bf16),
            pltpu.VMEM((rows // LANE, seeds, LANE), bf16),
            pltpu.VMEM((rows // LANE, seeds, LANE), bf16),
            pltpu.VMEM((rows, LANE), f32),
            pltpu.VMEM((seeds, LANE), f32),
            pltpu.VMEM((2 * blocks, 2 * depth, LANE), bf16),
            pltpu.VMEM((blocks, rows, 2 * LANE), f32),
            pltpu.VMEM((2 * blocks, rows, LANE), bf16),
            pltpu.SemaphoreType.DMA((n,)),
            pltpu.SemaphoreType.DMA((n,)),
            pltpu.SemaphoreType.DMA((n,)),
            pltpu.SemaphoreType.DMA((n,)),
            pltpu.SemaphoreType.DMA((n,)),
            pltpu.SemaphoreType.DMA((n,)),
            pltpu.SemaphoreType.DMA((2 * blocks,)),
            pltpu.SemaphoreType.DMA((2 * blocks,)),
            pltpu.SemaphoreType.DMA((10 + 2 * blocks,)),
            pltpu.SemaphoreType.DMA((n,)),
        ],
        compiler_params=pltpu.CompilerParams(
            collective_id=0, has_side_effects=True, vmem_limit_bytes=60 * 1024 * 1024
        ),
        name="sage",
    )(*args)


def solution(mesh):
    placed = (
        P("dom", "mp"),
        P(None, "mp"),
        P(),
        P(None, "mp"),
        P(),
        P("dom", None, None),
        P("dom", None),
        P("dom"),
        P("dom"),
        P("dom", None),
        P("dom"),
        P("dom"),
    )
    return jax.shard_map(
        functools.partial(shards, mesh.shape["dom"]),
        mesh=mesh, in_specs=placed, out_specs=P("dom", "mp"), check_vma=False,
    )
```

time: 61.7 us -> 60.3 us (0.977)
  Pallas kernels: 59.9 us -> 58.6 us
    pallas_call x1, Pallas kernels: 59.9 us -> 58.6 us  [shards(): pl.pallas_call(functools.partial(main_kernel, n), out_shape=jax.ShapeDtyp...]
where the time goes in v1:
time: 60.3 us; the launch traced here: 60.2 us
  Pallas kernels  58.6 us (97%)
  local copies, waits for them, and re-layouts  1.57 us (3%)
    pallas_call x1, Pallas kernels, shards(): pl.pallas_call(functools.partial(main_kernel, n), out_shape=jax.ShapeDtyp...  58.6 us
    unnamed x1, local copies, waits for them, and re-layouts  1.57 us

profile of v1, /device:TPU:0, one launch (start us, length us, event | category | flops | bytes accessed | tf_op | source)
XLA Modules:
  0.0 60.2 jit_solution(8208002791570607695)
XLA Ops:
  0.0 58.6 %sage.1 = bf16[256,256]{1,0:T(8,128)(2,1)} custom-call(s32[16,1,128]{2,1,0:T(1,128)} %bitcast.10, bf16[4096,384]{1,0:T(8,128)(2,1)} %table_any.1, s32[10,1024]{1,0:T(8,128)} %bitcast.9, s32[1,1024]{1,0:T(1,128)} %bitcast.12, s32[1,1024]{1,0:T(1,128)} %bitcast.13, s32[5,256]{1,0:T(8,128)} %bitcast.11, s32[1,256]{1,0:T(1,128)} %bitcast.16, s32[1,256]{1,0:T(1,128)} %bitcast.17, ...), custom_call_target="tpu_custom_call" | custom-call | tf_op jit(solution)/shard_map/sage/pallas_call | solution.py:361
  58.6 1.6 %copy.14 = bf16[256,256]{1,0:T(8,128)(2,1)} copy(bf16[256,256]{1,0:T(8,128)(2,1)} %sage.1) | data formatting | bytes 262144

commit v2 on v1

--- a/solution.py
+++ b/solution.py
@@ -12,7 +12,8 @@
 ANY = pl.BlockSpec(memory_space=pl.ANY)
 LANE = 128
 TILE = 256
-DEPTH = 256
+SPAN = 1024
+DEPTH = 128
 
 
 def bit(value, k):
@@ -29,10 +30,15 @@
     return me
 
 
-def mask_of(step, n):
-    half = lax.div(step, 2)
-    odd = lax.rem(step, 2)
-    return (1 - odd) * (n // 2 + half) + odd * (half + 1)
+def mask_of(step, n, outer):
+    half, quarter = n // 2, max(1, n // 4)
+
+    def near(at):
+        return at + quarter - lax.div(at, quarter) * (half - 1)
+
+    at, odd = lax.div(step, 2), lax.rem(step, 2)
+    mixed = (1 - odd) * (half + at) + odd * near(at)
+    return jnp.where(outer, jnp.where(step < half - 1, near(step), step + 1), mixed)
 
 
 def dot(a, b):
@@ -43,11 +49,11 @@
     return jnp.concatenate(pieces, axis=1)
 
 
-def index_rows(index, near_ref, own_ref, count_ref):
+def index_rows(index, near_ref, ints_ref):
     fan, rows = near_ref.shape
-    count = count_ref[...]
+    own, count = ints_ref[0], ints_ref[1]
     pieces = [jnp.where(count > j, near_ref[j : j + 1, :], -1) for j in range(fan)]
-    pieces += [own_ref[...], count, jnp.zeros((index.shape[1] - fan - 2, rows), jnp.int32)]
+    pieces += [own, count, jnp.zeros((index.shape[1] - fan - 2, rows), jnp.int32)]
     index[...] = jnp.concatenate(pieces, axis=0).T
 
 
@@ -84,7 +90,7 @@
     asked_any, table_any, near_a_any, self_a_any, count_a_any, near_b_any, self_b_any, count_b_any,
     weight_a_any, bias_a_any, weight_b_any, bias_b_any,
     out_ref,
-    asked, table, near_a, self_a, count_a, near_b, self_b, count_b, wa, bias_a, wb, bias_b,
+    asked, table, near_a, ints_a, near_b, ints_b, wa, wb, bias,
     wide, wanted, wanted_scalar, stage, found, index_a, index_b,
     fetched, sum_a, own_a, sum_b, own_b, inv_a, inv_b, mixed, total, hidden,
     ask_send, ask_recv, send_sem, recv_sem, relay_send, relay_recv, mp_send, mp_recv, load_sem, scalar_sem,
@@ -94,7 +100,7 @@
     partner = 1 - core
     flip = flips(me, n)
     cols, each = found.shape[1], found.shape[2]
-    rows, seeds, slots = inv_a.shape[0], inv_b.shape[0], n * each
+    rows, seeds = inv_a.shape[0], inv_b.shape[0]
     feature, hidden_width = wa.shape[1] // 2, wb.shape[1] // 2
     fan_a, fan_b = near_a.shape[0], near_b.shape[0]
     blocks = wa.shape[0] // 2
@@ -102,22 +108,27 @@
     groups = n // per
     depth = per * each
     deep = depth // LANE
+    mine = lax.div(me, per)
+    outer = bit(me, max(0, len(flip) - 1)) == bit(me, max(0, len(flip) - 2))
 
     def peer(step):
-        return exchanged(me, flip, mask_of(step, n))
-
-    loads = [
-        pltpu.make_async_copy(source, target, load_sem.at[i])
-        for i, (source, target) in enumerate(
-            [(asked_any, asked), (near_a_any, near_a), (self_a_any, self_a), (count_a_any, count_a),
-             (near_b_any, near_b), (self_b_any, self_b), (count_b_any, count_b), (table_any, table),
-             (bias_a_any, bias_a), (bias_b_any, bias_b)]
-            + [(weight_a_any.at[:, pl.ds(i * LANE, LANE)], wa.at[core * blocks + i]) for i in range(blocks)]
-            + [(weight_b_any.at[:, pl.ds(i * LANE, LANE)], wb.at[core * blocks + i]) for i in range(blocks)]
-        )
-    ]
-    for load in loads:
-        load.start()
+        return exchanged(me, flip, mask_of(step, n, outer))
+
+    own_blocks = pl.ds(core * blocks, blocks)
+    loads = []
+    for i, (target, sources) in enumerate([
+        (near_a, [near_a_any]), (ints_a, [self_a_any, count_a_any]),
+        (near_b, [near_b_any]), (ints_b, [self_b_any, count_b_any]), (asked, [asked_any]), (table, [table_any]),
+        (bias, [bias_a_any, bias_b_any]),
+        (wa.at[own_blocks], [weight_a_any.at[:, pl.ds(b * LANE, LANE)] for b in range(blocks)]),
+        (wb.at[own_blocks], [weight_b_any.at[:, pl.ds(b * LANE, LANE)] for b in range(blocks)]),
+    ]):
+        if len(sources) == 1:
+            pltpu.make_async_copy(sources[0], target, load_sem.at[i]).start()
+        else:
+            for b, source in enumerate(sources):
+                pltpu.make_async_copy(source, target.at[b], load_sem.at[i]).start()
+        loads.append(pltpu.make_async_copy(target, target, load_sem.at[i]))
 
     barrier = pltpu.get_barrier_semaphore()
 
@@ -128,28 +139,21 @@
     lax.fori_loop(0, n - 1, greet, 0)
     pl.semaphore_signal(barrier, inc=1, device_id={"mp": partner}, device_id_type=MESH)
 
-    for load in loads[1:7]:
-        load.wait()
-    index_rows(index_a, near_a, self_a, count_a)
-    index_rows(index_b, near_b, self_b, count_b)
-    steps = rows // 16
-    build_picks(index_a, fan_a, sum_a, own_a, inv_a, True, 0, steps // 2)
-
-    loads[0].wait()
+    loads[4].wait()
     wanted[me] = asked[me]
     pl.semaphore_wait(barrier, n)
 
     def ask(other):
         return pltpu.make_async_remote_copy(
             src_ref=asked.at[other], dst_ref=wanted.at[me],
-            send_sem=ask_send.at[other], recv_sem=ask_recv.at[me],
+            send_sem=ask_send, recv_sem=ask_recv.at[me],
             device_id={"dom": other}, device_id_type=MESH,
         )
 
     def give(other):
         return pltpu.make_async_remote_copy(
             src_ref=found.at[other], dst_ref=fetched.at[core, me],
-            send_sem=send_sem.at[other], recv_sem=recv_sem.at[me],
+            send_sem=send_sem, recv_sem=recv_sem.at[mine],
             device_id={"dom": other}, device_id_type=MESH,
         )
 
@@ -159,19 +163,26 @@
             device_id={"mp": partner}, device_id_type=MESH,
         )
 
-    def relay(other):
-        return over(fetched.at[core, other], fetched.at[core, other], relay_send.at[other], relay_recv.at[other])
+    def relay(group):
+        landed = fetched.at[core, pl.ds(group * per, per)]
+        return over(landed, landed, relay_send, relay_recv.at[group])
 
     def send_ask(step, carry):
         ask(peer(step)).start()
         return carry
 
     lax.fori_loop(0, n - 1, send_ask, 0)
-    for load in loads[7:]:
+    for load in loads[:4]:
+        load.wait()
+    index_rows(index_a, near_a, ints_a)
+    index_rows(index_b, near_b, ints_b)
+    steps = rows // 16
+    first = steps // 8
+
+    for load in loads[5:]:
         load.wait()
     shared = [
-        over(w.at[core * blocks + i], w.at[core * blocks + i], mp_send.at[s * blocks + i], mp_recv.at[s * blocks + i])
-        for s, w in enumerate((wa, wb)) for i in range(blocks)
+        over(w.at[own_blocks], w.at[own_blocks], mp_send.at[i], mp_recv.at[i]) for i, w in enumerate((wa, wb))
     ]
     for copy in shared:
         copy.start()
@@ -183,13 +194,13 @@
         return carry
 
     lax.fori_loop(0, table.shape[0] // 128, widen, 0)
-    build_picks(index_a, fan_a, sum_a, own_a, inv_a, True, steps // 2, steps)
-
-    def to_scalar(other):
-        return pltpu.make_async_copy(wanted.at[other], wanted_scalar.at[other], scalar_sem.at[other])
+    build_picks(index_a, fan_a, sum_a, own_a, inv_a, True, 0, first)
+
+    def to_scalar(other, step):
+        slot = scalar_sem.at[lax.rem(step, scalar_sem.shape[0])]
+        return pltpu.make_async_copy(wanted.at[other], wanted_scalar.at[other], slot)
 
     def find(other):
-        to_scalar(other).wait()
         for k in range(each):
             row = wanted_scalar[other, 0, k]
             for c in range(cols):
@@ -197,10 +208,10 @@
         for c in range(cols):
             found[other, c] = stage[c].astype(jnp.bfloat16)
 
-    behind = min(3, n)
+    behind = scalar_sem.shape[0] - 1
 
     def step_peer(step):
-        return exchanged(me, flip, jnp.where(step < n - 1, mask_of(step, n), 0))
+        return exchanged(me, flip, jnp.where(step < n - 1, mask_of(step, n, outer), 0))
 
     def find_and_send(step, carry):
         @pl.when(step < n)
@@ -211,11 +222,12 @@
             def _():
                 pltpu.make_async_copy(asked.at[other], wanted.at[other], ask_recv.at[other]).wait()
 
-            to_scalar(other).start()
+            to_scalar(other, step).start()
 
         @pl.when(step >= behind)
         def _():
             other = step_peer(step - behind)
+            to_scalar(other, step - behind).wait()
             find(other)
 
             @pl.when(step - behind < n - 1)
@@ -226,39 +238,36 @@
 
     lax.fori_loop(0, n + behind, find_and_send, 0)
     fetched[core, me] = found[me]
+    build_picks(index_a, fan_a, sum_a, own_a, inv_a, True, first, steps)
     build_picks(index_b, fan_b, sum_b, own_b, inv_b, False, 0, seeds // 16)
     total[...] = jnp.zeros_like(total)
-    relay(me).start()
     for copy in shared:
         copy.wait()
 
-    group_flip = flips(lax.div(me, per), groups)
-    half_groups = max(1, groups // 2)
+    group_flip = flips(mine, groups)
 
     def group_of(k):
-        j = lax.rem(k, 2) * half_groups + lax.div(k, 2)
-        return exchanged(lax.div(me, per), group_flip, j)
+        return exchanged(mine, group_flip, k)
 
     def take(group):
-        def arrive(i, carry):
-            other = group * per + i
-
-            @pl.when(other != me)
+        def arrived(count):
+            pltpu.make_async_copy(
+                found.at[pl.ds(0, count)], fetched.at[core, pl.ds(0, count)], recv_sem.at[group]
+            ).wait()
+
+        @pl.when(group != mine)
+        def _():
+            arrived(per)
+
+        if per > 1:
+            @pl.when(group == mine)
             def _():
-                pltpu.make_async_copy(found.at[other], fetched.at[core, other], recv_sem.at[other]).wait()
-                relay(other).start()
-
-            return carry
-
-        lax.fori_loop(0, per, arrive, 0)
+                arrived(per - 1)
+
+        relay(group).start()
 
     def use(group):
-        def arrive(i, carry):
-            other = group * per + i
-            pltpu.make_async_copy(found.at[other], fetched.at[partner, other], relay_recv.at[other]).wait()
-            return carry
-
-        lax.fori_loop(0, per, arrive, 0)
+        relay(group).wait_recv()
         lines = across([
             fetched[h, pl.ds(group * per, per), c].reshape(depth, LANE) for h in range(2) for c in range(cols)
         ])
@@ -270,13 +279,13 @@
                     mixed[b + i, which * depth : (which + 1) * depth, :] = value[:, i * LANE : (i + 1) * LANE]
 
         def one_tile(tile, carry):
-            at = pl.ds(pl.multiple_of(tile * TILE, TILE), TILE)
+            at = pl.ds(pl.multiple_of(tile * SPAN, SPAN), SPAN)
             picks = across([p[group * deep + i, at, :] for p in (own_a, sum_a) for i in range(deep)])
             for b in range(blocks):
                 total[b, at, :] += dot(picks, across([mixed[2 * b], mixed[2 * b + 1]]))
             return carry
 
-        lax.fori_loop(0, rows // TILE, one_tile, 0)
+        lax.fori_loop(0, rows // SPAN, one_tile, 0)
 
     def one_group(k, carry):
         @pl.when(k < groups)
@@ -297,7 +306,7 @@
         for b in range(blocks):
             for i in range(2):
                 cut = slice((2 * b + i) * LANE, (2 * b + i + 1) * LANE)
-                value = total[b, at, i * LANE : (i + 1) * LANE] * inverse + bias_a[:, cut]
+                value = total[b, at, i * LANE : (i + 1) * LANE] * inverse + bias[0, :, cut]
                 hidden[2 * b + i, at, :] = jnp.maximum(value, 0.0).astype(jnp.bfloat16)
         return carry
 
@@ -310,7 +319,7 @@
     mean = (mean * across([inv_b[...]] * (2 * blocks))).astype(jnp.bfloat16)
     state = dot(own, across([wb[b, :hidden_width] for b in range(2 * blocks)]))
     state = state + dot(mean, across([wb[b, hidden_width:] for b in range(2 * blocks)]))
-    state = jnp.maximum(state + bias_b[...], 0.0)
+    state = jnp.maximum(state + bias[1], 0.0)
     squares = jnp.sum(state * state, axis=1, keepdims=True)
     scale = jnp.sqrt(jnp.float32(hidden_width)) / jnp.sqrt(squares + hidden_width)
     state = (state * scale).astype(out_ref.dtype)
@@ -320,15 +329,10 @@
         def _():
             out_ref[...] = state[:, c * half : (c + 1) * half]
 
-    def finish(step, carry):
-        other = peer(step)
-        ask(other).wait_send()
-        give(other).wait_send()
-        relay(other).wait_send()
-        return carry
-
-    lax.fori_loop(0, n - 1, finish, 0)
-    relay(me).wait_send()
+    others = pl.ds(0, n - 1)
+    pltpu.make_async_copy(asked.at[others], wanted.at[others], ask_send).wait()
+    pltpu.make_async_copy(found.at[others], fetched.at[core, others], send_sem).wait()
+    pltpu.make_async_copy(fetched.at[core], fetched.at[partner], relay_send).wait()
 
 
 def shards(
@@ -352,7 +356,8 @@
     wide = -(-(near_a.shape[1] + 2) // 8) * 8
     bf16, f32 = jnp.bfloat16, jnp.float32
     cols, blocks = half // LANE, half_hidden // LANE
-    depth = max(1, DEPTH // each) * each
+    per = max(1, DEPTH // each)
+    depth, groups = per * each, n // per
     args = (
         requests[0][:, None, :], table,
         near_a.T, self_a[None, :], count_a[None, :], near_b.T, self_b[None, :], count_b[None, :],
@@ -360,14 +365,19 @@
     )
     return pl.pallas_call(
         functools.partial(main_kernel, n),
-        out_shape=jax.ShapeDtypeStruct((seeds, half_hidden), bf16),
+        out_shape=pltpu.VMEM((seeds, half_hidden), bf16),
         in_specs=[ANY] * len(args),
         out_specs=VMEM,
-        scratch_shapes=[pltpu.VMEM(a.shape, a.dtype) for a in args[:8]] + [
+        scratch_shapes=[
+            pltpu.VMEM(args[0].shape, jnp.int32),
+            pltpu.VMEM(table.shape, bf16),
+            pltpu.VMEM(args[2].shape, jnp.int32),
+            pltpu.VMEM((2, 1, rows), jnp.int32),
+            pltpu.VMEM(args[5].shape, jnp.int32),
+            pltpu.VMEM((2, 1, seeds), jnp.int32),
             pltpu.VMEM((2 * blocks, weight_a.shape[0], LANE), bf16),
-            pltpu.VMEM(args[9].shape, f32),
             pltpu.VMEM((2 * blocks, weight_b.shape[0], LANE), bf16),
-            pltpu.VMEM(args[11].shape, f32),
+            pltpu.VMEM((2, 1, bias_a.shape[0]), f32),
             pltpu.VMEM((cols, table.shape[0], LANE), f32),
             pltpu.VMEM((n, 1, each), jnp.int32),
             pltpu.SMEM((n, 1, each), jnp.int32),
@@ -385,16 +395,16 @@
             pltpu.VMEM((2 * blocks, 2 * depth, LANE), bf16),
             pltpu.VMEM((blocks, rows, 2 * LANE), f32),
             pltpu.VMEM((2 * blocks, rows, LANE), bf16),
+            pltpu.SemaphoreType.DMA,
             pltpu.SemaphoreType.DMA((n,)),
-            pltpu.SemaphoreType.DMA((n,)),
-            pltpu.SemaphoreType.DMA((n,)),
-            pltpu.SemaphoreType.DMA((n,)),
-            pltpu.SemaphoreType.DMA((n,)),
-            pltpu.SemaphoreType.DMA((n,)),
-            pltpu.SemaphoreType.DMA((2 * blocks,)),
-            pltpu.SemaphoreType.DMA((2 * blocks,)),
-            pltpu.SemaphoreType.DMA((10 + 2 * blocks,)),
-            pltpu.SemaphoreType.DMA((n,)),
+            pltpu.SemaphoreType.DMA,
+            pltpu.SemaphoreType.DMA((groups,)),
+            pltpu.SemaphoreType.DMA,
+            pltpu.SemaphoreType.DMA((groups,)),
+            pltpu.SemaphoreType.DMA((2,)),
+            pltpu.SemaphoreType.DMA((2,)),
+            pltpu.SemaphoreType.DMA((9,)),
+            pltpu.SemaphoreType.DMA((4,)),
         ],
         compiler_params=pltpu.CompilerParams(
             collective_id=0, has_side_effects=True, vmem_limit_bytes=60 * 1024 * 1024

time: 60.3 us -> 49 us (0.81); the launches traced: 60.2 us -> 48.1 us
  Pallas kernels: 58.6 us -> 47.4 us
  local copies, waits for them, and re-layouts: 1.57 us -> 0.66 us
    pallas_call x1, Pallas kernels: 58.6 us -> 47.4 us  [shards(): pl.pallas_call(functools.partial(main_kernel, n), out_shape=pltpu.VMEM((s...]
    unnamed x1, local copies, waits for them, and re-layouts: 1.57 us -> 0.66 us
where the time goes in v2:
time: 49 us; the launch traced here: 48.1 us
  Pallas kernels  47.4 us (97%)
  local copies, waits for them, and re-layouts  0.66 us (1%)
    pallas_call x1, Pallas kernels, shards(): pl.pallas_call(functools.partial(main_kernel, n), out_shape=pltpu.VMEM((s...  47.4 us

profile of v2, /device:TPU:0, one launch (start us, length us, event | category | flops | bytes accessed | tf_op | source)
XLA Modules:
  0.0 48.1 jit_solution(5230522379928481830)
XLA Ops:
  0.0 47.4 %sage.1 = bf16[256,256]{1,0:T(8,128)(2,1)S(1)} custom-call(s32[16,1,128]{2,1,0:T(1,128)} %bitcast.10, bf16[4096,384]{1,0:T(8,128)(2,1)} %table_any.1, s32[10,1024]{1,0:T(8,128)} %bitcast.9, s32[1,1024]{1,0:T(1,128)} %bitcast.12, s32[1,1024]{1,0:T(1,128)} %bitcast.13, s32[5,256]{1,0:T(8,128)} %bitcast.11, s32[1,256]{1,0:T(1,128)} %bitcast.16, ...), custom_call_target="tpu_custom_call" | custom-call | tf_op jit(solution)/shard_map/sage/pallas_call | solution.py:366
  47.4 0.7 %copy.14 = bf16[256,256]{1,0:T(8,128)(2,1)} copy(bf16[256,256]{1,0:T(8,128)(2,1)S(1)} %sage.1) | data formatting | bytes 262144

commit v3 on v2

--- a/solution.py
+++ b/solution.py
@@ -13,7 +13,8 @@
 LANE = 128
 TILE = 256
 SPAN = 1024
-DEPTH = 128
+PART = 4
+DEPTH = 256
 
 
 def bit(value, k):
@@ -30,15 +31,10 @@
     return me
 
 
-def mask_of(step, n, outer):
-    half, quarter = n // 2, max(1, n // 4)
-
-    def near(at):
-        return at + quarter - lax.div(at, quarter) * (half - 1)
-
-    at, odd = lax.div(step, 2), lax.rem(step, 2)
-    mixed = (1 - odd) * (half + at) + odd * near(at)
-    return jnp.where(outer, jnp.where(step < half - 1, near(step), step + 1), mixed)
+def mask_of(step, n):
+    half, quarter = n // 2, n // 4
+    crossing = half + quarter + lax.div(step, 2) - lax.rem(step, 2) * quarter
+    return jnp.where(step < half, crossing, step - half + 1)
 
 
 def dot(a, b):
@@ -57,29 +53,56 @@
     index[...] = jnp.concatenate(pieces, axis=0).T
 
 
-def build_picks(index_ref, fan, sum_pick, own_pick, inverse, scaled, first, last):
-    chunks = sum_pick.shape[0]
+def spread_matrix(width, fan):
+    shape = (2 * width, (fan + 2) * LANE)
+    line = lax.broadcasted_iota(jnp.int32, shape, 0)
+    block = lax.broadcasted_iota(jnp.int32, shape, 1) >> 7
+    high = jnp.where(line == block, 128.0, 0.0)
+    return jnp.where(line == block + width, 1.0, high).astype(jnp.bfloat16)
+
+
+def spread_index(index_ref, matrix, spread, inverse, weight):
+    rows = index_ref.shape[0]
+    fan = spread.shape[0] - 1
+    size = min(rows, TILE)
+
+    def one(at, carry):
+        r0 = pl.ds(pl.multiple_of(at * size, size), size)
+        index = index_ref[r0, :]
+        parts = across([index >> 7, index & 127]).astype(jnp.float32).astype(jnp.bfloat16)
+        for j in range(0, fan + 2, 2):
+            wide = dot(parts, matrix[:, j * LANE : min(j + 2, fan + 2) * LANE])
+            for i in range(min(2, fan + 2 - j)):
+                value = wide[:, i * LANE : (i + 1) * LANE]
+                if j + i <= fan:
+                    spread[j + i, r0, :] = value.astype(jnp.int32)
+                else:
+                    inverse[r0, :] = 1.0 / value
+                    if weight is not None:
+                        weight[r0, :] = value
+        return carry
+
+    lax.fori_loop(0, rows // size, one, 0)
+
+
+def build_picks(spread, weight, sum_pick, own_pick, start, chunks, base, first, last):
+    fan = spread.shape[0] - 1
     high = 16
 
     def one(at, carry):
-        r0 = pl.multiple_of(at * high, high)
-        index = index_ref[pl.ds(r0, high), :]
-        lanes = [
-            jnp.broadcast_to(index[:, j : j + 1], (high, LANE)).astype(jnp.int16)
-            for j in range(fan + 1)
-        ]
-        count = jnp.broadcast_to(index[:, fan + 1 : fan + 2], (high, LANE)).astype(jnp.float32)
-        inverse[pl.ds(r0, high), :] = 1.0 / count
-        lane = lax.broadcasted_iota(jnp.int32, (high, LANE), 1)
-        one_value, no_value = jnp.bfloat16(1.0), jnp.bfloat16(0.0)
-        own_value = count.astype(jnp.bfloat16) if scaled else one_value
-        for c in range(chunks):
-            column = (lane + c * LANE).astype(jnp.int16)
-            total = jnp.where(lanes[0] == column, one_value, no_value)
-            for j in range(1, fan):
-                total = total + jnp.where(lanes[j] == column, one_value, no_value)
-            sum_pick[c, pl.ds(r0, high), :] = total
-            own_pick[c, pl.ds(r0, high), :] = jnp.where(lanes[fan] == column, own_value, no_value)
+        for part in range(PART):
+            r0 = pl.ds(pl.multiple_of((at * PART + part) * high, high), high)
+            lanes = [spread[j, r0, :].astype(jnp.int16) for j in range(fan + 1)]
+            lane = lax.broadcasted_iota(jnp.int32, (high, LANE), 1) + base
+            one_value, no_value = jnp.bfloat16(1.0), jnp.bfloat16(0.0)
+            own_value = one_value if weight is None else weight[r0, :].astype(jnp.bfloat16)
+            for c in range(chunks):
+                column = (lane + c * LANE).astype(jnp.int16)
+                total = jnp.where(lanes[0] == column, one_value, no_value)
+                for j in range(1, fan):
+                    total = total + jnp.where(lanes[j] == column, one_value, no_value)
+                sum_pick[start + c, r0, :] = total
+                own_pick[start + c, r0, :] = jnp.where(lanes[fan] == column, own_value, no_value)
         return carry
 
     lax.fori_loop(first, last, one, 0)
@@ -92,8 +115,11 @@
     out_ref,
     asked, table, near_a, ints_a, near_b, ints_b, wa, wb, bias,
     wide, wanted, wanted_scalar, stage, found, index_a, index_b,
-    fetched, sum_a, own_a, sum_b, own_b, inv_a, inv_b, mixed, total, hidden,
+    fetched, helped, near_h, ints_h, matrix_a, matrix_b, spread, spread_b, weight, sum_a, own_a, sum_h, own_h, sum_b, own_b,
+    inv_a, inv_b, mixed, total, mixed_h, total_h, part_out, part_in, hidden,
     ask_send, ask_recv, send_sem, recv_sem, relay_send, relay_recv, mp_send, mp_recv, load_sem, scalar_sem,
+    index_send, index_recv, help_recv, help_relay_send, help_relay_recv,
+    part_send, part_recv, part_relay_send, part_relay_recv,
 ):
     me = lax.axis_index("dom")
     core = lax.axis_index("mp")
@@ -109,10 +135,17 @@
     depth = per * each
     deep = depth // LANE
     mine = lax.div(me, per)
-    outer = bit(me, max(0, len(flip) - 1)) == bit(me, max(0, len(flip) - 2))
+    half, half_groups = n // 2, groups // 2
+    half_chunks = sum_a.shape[0] // 2
+    outer = bit(me, len(flip) - 1) == bit(me, len(flip) - 2)
+    inner = bit(me, len(flip) - 1) != bit(me, len(flip) - 2)
+    twin = exchanged(me, flip, half + half // 2)
+    here = lax.rem(me, half)
+    near_base = bit(me, len(flip) - 1) * (half_chunks * LANE)
+    far_base = half_chunks * LANE - near_base
 
     def peer(step):
-        return exchanged(me, flip, mask_of(step, n, outer))
+        return exchanged(me, flip, mask_of(step, n))
 
     own_blocks = pl.ds(core * blocks, blocks)
     loads = []
@@ -157,6 +190,19 @@
             device_id={"dom": other}, device_id_type=MESH,
         )
 
+    def lend(source, helper):
+        return pltpu.make_async_remote_copy(
+            src_ref=found.at[source], dst_ref=helped.at[core, here],
+            send_sem=send_sem, recv_sem=help_recv.at[lax.div(here, per)],
+            device_id={"dom": helper}, device_id_type=MESH,
+        )
+
+    def to_twin(source, target, send, recv):
+        return pltpu.make_async_remote_copy(
+            src_ref=source, dst_ref=target, send_sem=send, recv_sem=recv,
+            device_id={"dom": twin}, device_id_type=MESH,
+        )
+
     def over(source, target, send, recv):
         return pltpu.make_async_remote_copy(
             src_ref=source, dst_ref=target, send_sem=send, recv_sem=recv,
@@ -174,10 +220,16 @@
     lax.fori_loop(0, n - 1, send_ask, 0)
     for load in loads[:4]:
         load.wait()
-    index_rows(index_a, near_a, ints_a)
     index_rows(index_b, near_b, ints_b)
-    steps = rows // 16
-    first = steps // 8
+    index_copies = [
+        to_twin(near_a, near_h, index_send.at[0], index_recv.at[0]),
+        to_twin(ints_a, ints_h, index_send.at[1], index_recv.at[1]),
+    ]
+
+    @pl.when(outer)
+    def _():
+        for copy in index_copies:
+            copy.start()
 
     for load in loads[5:]:
         load.wait()
@@ -194,7 +246,9 @@
         return carry
 
     lax.fori_loop(0, table.shape[0] // 128, widen, 0)
-    build_picks(index_a, fan_a, sum_a, own_a, inv_a, True, 0, first)
+    matrix_a[...] = spread_matrix(index_a.shape[1], fan_a)
+    matrix_b[...] = spread_matrix(index_b.shape[1], fan_b)
+    steps = rows // (16 * PART)
 
     def to_scalar(other, step):
         slot = scalar_sem.at[lax.rem(step, scalar_sem.shape[0])]
@@ -211,7 +265,7 @@
     behind = scalar_sem.shape[0] - 1
 
     def step_peer(step):
-        return exchanged(me, flip, jnp.where(step < n - 1, mask_of(step, n, outer), 0))
+        return exchanged(me, flip, jnp.where(step < n - 1, mask_of(step, n), 0))
 
     def find_and_send(step, carry):
         @pl.when(step < n)
@@ -230,43 +284,62 @@
             to_scalar(other, step - behind).wait()
             find(other)
 
-            @pl.when(step - behind < n - 1)
+            mask = mask_of(step - behind, n)
+            low = half + jnp.where(outer, half // 2, 0)
+            lent = (mask >= low) & (mask < low + half // 2)
+
+            hop = mask - low + jnp.where(outer, 0, half // 2)
+
+            @pl.when((step - behind < half) & lent & (hop == 0))
+            def _():
+                helped[core, here] = found[other]
+
+            @pl.when((step - behind < half) & lent & (hop != 0))
+            def _():
+                lend(other, exchanged(me, flip, hop)).start()
+
+            @pl.when((step - behind < half) & jnp.logical_not(lent))
             def _():
                 give(other).start()
 
+        return carry
+
+    def give_near(mask, carry):
+        give(exchanged(me, flip, mask)).start()
         return carry
 
     lax.fori_loop(0, n + behind, find_and_send, 0)
     fetched[core, me] = found[me]
-    build_picks(index_a, fan_a, sum_a, own_a, inv_a, True, first, steps)
-    build_picks(index_b, fan_b, sum_b, own_b, inv_b, False, 0, seeds // 16)
-    total[...] = jnp.zeros_like(total)
+
     for copy in shared:
         copy.wait()
 
     group_flip = flips(mine, groups)
 
+    def turn_of(k):
+        quarter = groups // 4
+        turned = (3 - lax.div(k, quarter)) * quarter + lax.rem(k, quarter)
+        return jnp.where(outer, k, turned)
+
     def group_of(k):
-        return exchanged(mine, group_flip, k)
+        return exchanged(mine, group_flip, turn_of(k))
+
+    def arrived(count, sem):
+        pltpu.make_async_copy(found.at[pl.ds(0, count)], fetched.at[core, pl.ds(0, count)], sem).wait()
 
     def take(group):
-        def arrived(count):
-            pltpu.make_async_copy(
-                found.at[pl.ds(0, count)], fetched.at[core, pl.ds(0, count)], recv_sem.at[group]
-            ).wait()
-
         @pl.when(group != mine)
         def _():
-            arrived(per)
+            arrived(per, recv_sem.at[group])
 
         if per > 1:
             @pl.when(group == mine)
             def _():
-                arrived(per - 1)
+                arrived(per - 1, recv_sem.at[group])
 
         relay(group).start()
 
-    def use(group):
+    def use(group, chunk):
         relay(group).wait_recv()
         lines = across([
             fetched[h, pl.ds(group * per, per), c].reshape(depth, LANE) for h in range(2) for c in range(cols)
@@ -280,37 +353,152 @@
 
         def one_tile(tile, carry):
             at = pl.ds(pl.multiple_of(tile * SPAN, SPAN), SPAN)
-            picks = across([p[group * deep + i, at, :] for p in (own_a, sum_a) for i in range(deep)])
+            picks = across([p[chunk + i, at, :] for p in (own_a, sum_a) for i in range(deep)])
             for b in range(blocks):
                 total[b, at, :] += dot(picks, across([mixed[2 * b], mixed[2 * b + 1]]))
             return carry
 
         lax.fori_loop(0, rows // SPAN, one_tile, 0)
 
+    def help_relay(group):
+        landed = helped.at[core, pl.ds(group * per, per)]
+        return over(landed, landed, help_relay_send, help_relay_recv.at[group])
+
+    def help_take(group):
+        @pl.when(group != lax.div(here, per))
+        def _():
+            arrived(per, help_recv.at[group])
+
+        if per > 1:
+            @pl.when(group == lax.div(here, per))
+            def _():
+                arrived(per - 1, help_recv.at[group])
+
+        help_relay(group).start()
+
+    def help_use(group):
+        help_relay(group).wait_recv()
+        lines = across([
+            helped[h, pl.ds(group * per, per), c].reshape(depth, LANE) for h in range(2) for c in range(cols)
+        ])
+        for which in range(2):
+            at = pl.ds(which * feature, feature)
+            value = dot(lines, across([wa[core * blocks + i, at, :] for i in range(blocks)])).astype(jnp.bfloat16)
+            for i in range(blocks):
+                mixed_h[i, which * depth : (which + 1) * depth, :] = value[:, i * LANE : (i + 1) * LANE]
+
+        def one_tile(tile, carry):
+            at = pl.ds(pl.multiple_of(tile * SPAN, SPAN), SPAN)
+            picks = across([p[group * deep + i, at, :] for p in (own_h, sum_h) for i in range(deep)])
+            total_h[at, :] += dot(picks, across([mixed_h[i] for i in range(blocks)]))
+            return carry
+
+        lax.fori_loop(0, rows // SPAN, one_tile, 0)
+
+    tiles = rows // TILE
+
+    def part_copy(tile):
+        return to_twin(
+            part_out.at[tile], part_in.at[core, tile], part_send, part_recv.at[tile]
+        )
+
+    def part_relay(tile):
+        landed = part_in.at[core, tile]
+        return over(landed, landed, part_relay_send, part_relay_recv.at[tile])
+
+    @pl.when(outer)
+    def _():
+        for copy in index_copies:
+            copy.wait_recv()
+        index_rows(index_a, near_h, ints_h)
+        total_h[...] = jnp.zeros_like(total_h)
+        spread_index(index_a, matrix_a, spread, inv_a, weight)
+        build_picks(spread, weight, sum_h, own_h, 0, half_chunks, near_base, 0, steps)
+        lax.fori_loop(1, half, give_near, 0)
+
+        def one_help(k, carry):
+            @pl.when(k < half_groups)
+            def _():
+                help_take(k)
+
+            @pl.when(k > 0)
+            def _():
+                help_use(k - 1)
+
+            return carry
+
+        lax.fori_loop(0, half_groups + 1, one_help, 0)
+
+        def put(tile, carry):
+            at = pl.ds(pl.multiple_of(tile * TILE, TILE), TILE)
+            for i in range(blocks):
+                part_out[tile, i] = total_h[at, i * LANE : (i + 1) * LANE].astype(jnp.bfloat16)
+            part_copy(tile).start()
+            return carry
+
+        lax.fori_loop(0, tiles, put, 0)
+
+    index_rows(index_a, near_a, ints_a)
+    spread_index(index_a, matrix_a, spread, inv_a, weight)
+    build_picks(spread, weight, sum_a, own_a, 0, half_chunks, near_base, 0, steps)
+
+    @pl.when(inner)
+    def _():
+        lax.fori_loop(1, half, give_near, 0)
+        build_picks(spread, weight, sum_a, own_a, half_chunks, half_chunks, far_base, 0, steps)
+
+    spread_index(index_b, matrix_b, spread_b, inv_b, None)
+    build_picks(spread_b, None, sum_b, own_b, 0, own_b.shape[0], 0, 0, seeds // (16 * PART))
+    total[...] = jnp.zeros_like(total)
+    live_groups = jnp.where(outer, half_groups, groups)
+
     def one_group(k, carry):
-        @pl.when(k < groups)
+        @pl.when(k < live_groups)
         def _():
             take(group_of(k))
 
         @pl.when(k > 0)
         def _():
-            use(group_of(k - 1))
-
-        return carry
-
-    lax.fori_loop(0, groups + 1, one_group, 0)
-
-    def hide(tile, carry):
+            group = group_of(k - 1)
+            far = lax.div(turn_of(k - 1), half_groups)
+            use(group, (lax.rem(group, half_groups) + far * half_groups) * deep)
+
+        return carry
+
+    lax.fori_loop(0, live_groups + 1, one_group, 0)
+
+    def hide(tile, parts):
         at = pl.ds(pl.multiple_of(tile * TILE, TILE), TILE)
         inverse = inv_a[at, :]
-        for b in range(blocks):
-            for i in range(2):
-                cut = slice((2 * b + i) * LANE, (2 * b + i + 1) * LANE)
-                value = total[b, at, i * LANE : (i + 1) * LANE] * inverse + bias[0, :, cut]
-                hidden[2 * b + i, at, :] = jnp.maximum(value, 0.0).astype(jnp.bfloat16)
-        return carry
-
-    lax.fori_loop(0, rows // TILE, hide, 0)
+        for b in range(2 * blocks):
+            value = total[b // 2, at, (b % 2) * LANE : (b % 2 + 1) * LANE]
+            if parts:
+                value = value + part_in[b // blocks, tile, b % blocks].astype(jnp.float32)
+            value = value * inverse + bias[0, :, b * LANE : (b + 1) * LANE]
+            hidden[b, at, :] = jnp.maximum(value, 0.0).astype(jnp.bfloat16)
+
+    @pl.when(inner)
+    def _():
+        def plain(tile, carry):
+            hide(tile, False)
+            return carry
+
+        lax.fori_loop(0, tiles, plain, 0)
+
+    @pl.when(outer)
+    def _():
+        def pass_on(tile, carry):
+            part_copy(tile).wait_recv()
+            part_relay(tile).start()
+            return carry
+
+        def joined(tile, carry):
+            part_relay(tile).wait_recv()
+            hide(tile, True)
+            return carry
+
+        lax.fori_loop(0, tiles, pass_on, 0)
+        lax.fori_loop(0, tiles, joined, 0)
 
     hidden_all = across([hidden[b] for b in range(2 * blocks)])
     chunks_b = own_b.shape[0]
@@ -323,16 +511,29 @@
     squares = jnp.sum(state * state, axis=1, keepdims=True)
     scale = jnp.sqrt(jnp.float32(hidden_width)) / jnp.sqrt(squares + hidden_width)
     state = (state * scale).astype(out_ref.dtype)
-    half = out_ref.shape[1]
+    width = out_ref.shape[1]
     for c in range(2):
         @pl.when(core == c)
         def _():
-            out_ref[...] = state[:, c * half : (c + 1) * half]
+            out_ref[...] = state[:, c * width : (c + 1) * width]
 
     others = pl.ds(0, n - 1)
     pltpu.make_async_copy(asked.at[others], wanted.at[others], ask_send).wait()
-    pltpu.make_async_copy(found.at[others], fetched.at[core, others], send_sem).wait()
-    pltpu.make_async_copy(fetched.at[core], fetched.at[partner], relay_send).wait()
+
+    @pl.when(outer)
+    def _():
+        for copy in index_copies:
+            copy.wait_send()
+        arrived(n - 2, send_sem)
+        arrived(half, relay_send)
+        arrived(half, help_relay_send)
+        pltpu.make_async_copy(part_out, part_in.at[core], part_send).wait()
+        pltpu.make_async_copy(part_in.at[core], part_in.at[partner], part_relay_send).wait()
+
+    @pl.when(inner)
+    def _():
+        arrived(n - 1, send_sem)
+        arrived(n, relay_send)
 
 
 def shards(
@@ -386,14 +587,28 @@
             pltpu.VMEM((rows, wide), jnp.int32),
             pltpu.VMEM((seeds, wide), jnp.int32),
             pltpu.VMEM((2, n, cols, each, LANE), bf16),
+            pltpu.VMEM((2, n // 2, cols, each, LANE), bf16),
+            pltpu.VMEM(args[2].shape, jnp.int32),
+            pltpu.VMEM((2, 1, rows), jnp.int32),
+            pltpu.VMEM((2 * wide, (near_a.shape[1] + 2) * LANE), bf16),
+            pltpu.VMEM((2 * wide, (near_b.shape[1] + 2) * LANE), bf16),
+            pltpu.VMEM((near_a.shape[1] + 1, rows, LANE), jnp.int32),
+            pltpu.VMEM((near_b.shape[1] + 1, seeds, LANE), jnp.int32),
+            pltpu.VMEM((rows, LANE), f32),
             pltpu.VMEM((slots // LANE, rows, LANE), bf16),
             pltpu.VMEM((slots // LANE, rows, LANE), bf16),
+            pltpu.VMEM((slots // LANE // 2, rows, LANE), bf16),
+            pltpu.VMEM((slots // LANE // 2, rows, LANE), bf16),
             pltpu.VMEM((rows // LANE, seeds, LANE), bf16),
             pltpu.VMEM((rows // LANE, seeds, LANE), bf16),
             pltpu.VMEM((rows, LANE), f32),
             pltpu.VMEM((seeds, LANE), f32),
             pltpu.VMEM((2 * blocks, 2 * depth, LANE), bf16),
             pltpu.VMEM((blocks, rows, 2 * LANE), f32),
+            pltpu.VMEM((blocks, 2 * depth, LANE), bf16),
+            pltpu.VMEM((rows, half_hidden), f32),
+            pltpu.VMEM((rows // TILE, blocks, TILE, LANE), bf16),
+            pltpu.VMEM((2, rows // TILE, blocks, TILE, LANE), bf16),
             pltpu.VMEM((2 * blocks, rows, LANE), bf16),
             pltpu.SemaphoreType.DMA,
             pltpu.SemaphoreType.DMA((n,)),
@@ -405,6 +620,15 @@
             pltpu.SemaphoreType.DMA((2,)),
             pltpu.SemaphoreType.DMA((9,)),
             pltpu.SemaphoreType.DMA((4,)),
+            pltpu.SemaphoreType.DMA((2,)),
+            pltpu.SemaphoreType.DMA((2,)),
+            pltpu.SemaphoreType.DMA((groups // 2,)),
+            pltpu.SemaphoreType.DMA,
+            pltpu.SemaphoreType.DMA((groups // 2,)),
+            pltpu.SemaphoreType.DMA,
+            pltpu.SemaphoreType.DMA((rows // TILE,)),
+            pltpu.SemaphoreType.DMA,
+            pltpu.SemaphoreType.DMA((rows // TILE,)),
         ],
         compiler_params=pltpu.CompilerParams(
             collective_id=0, has_side_effects=True, vmem_limit_bytes=60 * 1024 * 1024

time: 49 us -> 45.6 us (0.931)
  Pallas kernels: 47.4 us -> 44.3 us
    pallas_call x1, Pallas kernels: 47.4 us -> 44.3 us  [shards(): pl.pallas_call(functools.partial(main_kernel, n), out_shape=pltpu.VMEM((s...]
where the time goes in v3:
time: 45.6 us; the launch traced here: 45 us
  Pallas kernels  44.3 us (97%)
  local copies, waits for them, and re-layouts  0.66 us (1%)
    pallas_call x1, Pallas kernels, shards(): pl.pallas_call(functools.partial(main_kernel, n), out_shape=pltpu.VMEM((s...  44.3 us

profile of v3, /device:TPU:0, one launch (start us, length us, event | category | flops | bytes accessed | tf_op | source)
XLA Modules:
  0.0 45.0 jit_solution(3518698300543281452)
XLA Ops:
  0.0 44.3 %sage.1 = bf16[256,256]{1,0:T(8,128)(2,1)S(1)} custom-call(s32[16,1,128]{2,1,0:T(1,128)} %bitcast.10, bf16[4096,384]{1,0:T(8,128)(2,1)} %table_any.1, s32[10,1024]{1,0:T(8,128)} %bitcast.9, s32[1,1024]{1,0:T(1,128)} %bitcast.12, s32[1,1024]{1,0:T(1,128)} %bitcast.13, s32[5,256]{1,0:T(8,128)} %bitcast.11, s32[1,256]{1,0:T(1,128)} %bitcast.16, ...), custom_call_target="tpu_custom_call" | custom-call | tf_op jit(solution)/shard_map/sage/pallas_call | solution.py:567
  44.3 0.7 %copy.14 = bf16[256,256]{1,0:T(8,128)(2,1)} copy(bf16[256,256]{1,0:T(8,128)(2,1)S(1)} %sage.1) | data formatting | bytes 262144

commit v4 on v3

--- a/solution.py
+++ b/solution.py
@@ -31,10 +31,13 @@
     return me
 
 
-def mask_of(step, n):
+def mask_of(step, n, outer):
     half, quarter = n // 2, n // 4
-    crossing = half + quarter + lax.div(step, 2) - lax.rem(step, 2) * quarter
-    return jnp.where(step < half, crossing, step - half + 1)
+    odd = lax.rem(step, 2)
+    first = half + quarter + lax.div(step, 2) - odd * jnp.where(outer, half, quarter)
+    at = step - half
+    crossing = jnp.where(at < quarter, half + at, at - quarter + 1)
+    return jnp.where(step < half, first, jnp.where(outer, crossing, at + 1))
 
 
 def dot(a, b):
@@ -145,7 +148,7 @@
     far_base = half_chunks * LANE - near_base
 
     def peer(step):
-        return exchanged(me, flip, mask_of(step, n))
+        return exchanged(me, flip, mask_of(step, n, outer))
 
     own_blocks = pl.ds(core * blocks, blocks)
     loads = []
@@ -265,7 +268,7 @@
     behind = scalar_sem.shape[0] - 1
 
     def step_peer(step):
-        return exchanged(me, flip, jnp.where(step < n - 1, mask_of(step, n), 0))
+        return exchanged(me, flip, jnp.where(step < n - 1, mask_of(step, n, outer), 0))
 
     def find_and_send(step, carry):
         @pl.when(step < n)
@@ -284,7 +287,7 @@
             to_scalar(other, step - behind).wait()
             find(other)
 
-            mask = mask_of(step - behind, n)
+            mask = mask_of(step - behind, n, outer)
             low = half + jnp.where(outer, half // 2, 0)
             lent = (mask >= low) & (mask < low + half // 2)
 
@@ -298,7 +301,7 @@
             def _():
                 lend(other, exchanged(me, flip, hop)).start()
 
-            @pl.when((step - behind < half) & jnp.logical_not(lent))
+            @pl.when((step - behind < half + jnp.where(outer, half // 2, 0)) & jnp.logical_not(lent))
             def _():
                 give(other).start()
 
@@ -414,7 +417,7 @@
         total_h[...] = jnp.zeros_like(total_h)
         spread_index(index_a, matrix_a, spread, inv_a, weight)
         build_picks(spread, weight, sum_h, own_h, 0, half_chunks, near_base, 0, steps)
-        lax.fori_loop(1, half, give_near, 0)
+        lax.fori_loop(1, half // 2, give_near, 0)
 
         def one_help(k, carry):
             @pl.when(k < half_groups)

time: 45.6 us -> 45.4 us (level)
  no operation moved by 1% of the time
where the time goes in v4:
time: 45.4 us; the launch traced here: 44.7 us
  Pallas kernels  44 us (97%)
  local copies, waits for them, and re-layouts  0.66 us (1%)
    pallas_call x1, Pallas kernels, shards(): pl.pallas_call(functools.partial(main_kernel, n), out_shape=pltpu.VMEM((s...  44 us

profile of v4, /device:TPU:0, one launch (start us, length us, event | category | flops | bytes accessed | tf_op | source)
XLA Modules:
  0.0 44.7 jit_solution(244103297553333571)
XLA Ops:
  0.0 44.0 %sage.1 = bf16[256,256]{1,0:T(8,128)(2,1)S(1)} custom-call(s32[16,1,128]{2,1,0:T(1,128)} %bitcast.10, bf16[4096,384]{1,0:T(8,128)(2,1)} %table_any.1, s32[10,1024]{1,0:T(8,128)} %bitcast.9, s32[1,1024]{1,0:T(1,128)} %bitcast.12, s32[1,1024]{1,0:T(1,128)} %bitcast.13, s32[5,256]{1,0:T(8,128)} %bitcast.11, s32[1,256]{1,0:T(1,128)} %bitcast.16, ...), custom_call_target="tpu_custom_call" | custom-call | tf_op jit(solution)/shard_map/sage/pallas_call | solution.py:570
  44.0 0.7 %copy.14 = bf16[256,256]{1,0:T(8,128)(2,1)} copy(bf16[256,256]{1,0:T(8,128)(2,1)S(1)} %sage.1) | data formatting | bytes 262144
